TPU v7x, 32 devices: a whole 2x2x4 slice. The times are simulated.
32 devices in a mesh: tok: 4 (over y, x), hid: 2 (over core), voc: 4 (over z).
Axes of the slice: x: 2, y: 2, z: 4, core: 2. Of those that a mesh axis runs over, the one named last changes fastest.
Arguments:
- student_hidden: bfloat16 [512, 8192], P('tok', ('hid', 'voc')), may hold values from -8 to 8
- teacher_hidden: bfloat16 [512, 16384], P('tok', ('hid', 'voc')), may hold values from -8 to 8
- student_head: bfloat16 [8192, 2048], P('hid', 'voc'), may hold values from -2 to 2
- teacher_head: bfloat16 [16384, 2048], P('hid', 'voc'), may hold values from -2 to 2
- loss_weight: float32 [512], P('tok'), may hold values from 128 to 1024
Outputs:
- grad_hidden: bfloat16 [512, 8192], P('tok', ('hid', 'voc'))
- mean_loss: float32 [], replicated
All inputs are finite; a program needn't handle non-finite values.
Results may differ from a plain program's by a relative error of at most 0.001.
The roundings to bfloat16 on the way count: a program that leaves them out, or rounds other values in their place, can miss the bound.
Values may be sent and summed in bfloat16 or wider, within the bound.
A program may use at most 64 MiB of HBM per device.

v0:
```python
import jax
import jax.numpy as jnp
from jax import lax
from jax.sharding import PartitionSpec as P


def divergence_terms(student_logits, teacher_logits, weights):
    differences = teacher_logits - student_logits
    peak_student, peak_teacher = lax.pmax(
        (jnp.max(student_logits, axis=1), jnp.max(teacher_logits, axis=1)), "voc"
    )
    scaled_student = jnp.exp(student_logits - peak_student[:, None])
    scaled_teacher = jnp.exp(teacher_logits - peak_teacher[:, None])
    total_student, total_teacher, cross_sum = lax.psum(
        (
            jnp.sum(scaled_student, axis=1),
            jnp.sum(scaled_teacher, axis=1),
            jnp.sum(scaled_teacher * differences, axis=1),
        ),
        "voc",
    )
    student_lse = peak_student + jnp.log(total_student)
    teacher_lse = peak_teacher + jnp.log(total_teacher)
    divergence = cross_sum / total_teacher - teacher_lse + student_lse
    prob_gap = jnp.exp(student_logits - student_lse[:, None]) - jnp.exp(
        teacher_logits - teacher_lse[:, None]
    )
    scaled_gap = (weights[:, None] * prob_gap).astype(jnp.bfloat16)
    return (divergence, scaled_gap)


def shards(student_hidden, teacher_hidden, student_head, teacher_head, loss_weight):
    student_block, teacher_block = (
        lax.all_gather(student_hidden, "voc", axis=1, tiled=True),
        lax.all_gather(teacher_hidden, "voc", axis=1, tiled=True),
    )
    vocab_local = student_head.shape[1]
    row_count = student_block.shape[0] // lax.axis_size("hid")
    joined = lax.psum_scatter(
        jnp.concatenate(
            [
                jnp.dot(student_block, student_head, preferred_element_type=jnp.float32),
                jnp.dot(teacher_block, teacher_head, preferred_element_type=jnp.float32),
            ],
            axis=1,
        ),
        "hid",
        scatter_dimension=0,
        tiled=True,
    )
    student_logits = joined[:, :vocab_local]
    teacher_logits = joined[:, vocab_local:]
    weights = lax.dynamic_slice_in_dim(loss_weight, lax.axis_index("hid") * row_count, row_count)
    divergence, scaled_gap = divergence_terms(student_logits, teacher_logits, weights)
    token_total = loss_weight.shape[0] * lax.axis_size("tok")
    loss_total = lax.psum(jnp.sum(divergence), ("tok", "hid"))
    grad_terms = lax.dot_general(
        lax.all_gather(scaled_gap, "hid", axis=0, tiled=True),
        student_head,
        (((1,), (1,)), ((), ())),
        preferred_element_type=jnp.float32,
    )
    grad_hidden = lax.psum_scatter(grad_terms, "voc", scatter_dimension=1, tiled=True).astype(
        jnp.bfloat16
    )
    mean_loss = loss_total / token_total
    return (grad_hidden, mean_loss)


def solution(mesh):
    placed = (
        P("tok", ("hid", "voc")),
        P("tok", ("hid", "voc")),
        P("hid", "voc"),
        P("hid", "voc"),
        P("tok"),
    )
    return jax.shard_map(
        shards,
        mesh=mesh,
        in_specs=placed,
        out_specs=(P("tok", ("hid", "voc")), P()),
        check_vma=False,
    )
```

profile of v0, /device:TPU:0, one launch (start us, length us, event | category | flops | bytes accessed | tf_op | source)
XLA Modules:
  0.0 184.0 jit_solution(341071947678527449)
XLA Ops:
  7.2 0.0 all-gather.3.cloned.1.call-start
  7.2 0.7 all-gather.3.cloned.1.call-update
  7.9 0.0 all-gather.5.cloned.1.call-start
  7.9 0.7 all-gather.5.cloned.1.call-update
  8.6 0.0 reduce-scatter.3.cloned.1.call-start
  8.7 31.6 %all-gather.3.cloned.1.call-done = bf16[128,4096]{1,0:T(8,128)(2,1)} async-done(((bf16[128,1024]{1,0:T(8,128)(2,1)}), bf16[128,4096]{1,0:T(8,128)(2,1)}) %all-gather.3.cloned.1.call-update) | async-done | bytes 1048592 | tf_op jit(solution)/shard_map/all_gather | solution.py:34
  40.3 3.2 %fusion.1 = f32[128,512]{1,0:T(8,128)S(1)} fusion(bf16[128,4096]{1,0:T(8,128)(2,1)} %all-gather.3.cloned.1.call-done, bf16[4096,512]{1,0:T(8,128)(2,1)} %param.7), kind=kOutput, calls=%fused_computation.11 | convolution fusion | flops 536870912 | bytes 5505024 | tf_op jit(solution)/shard_map/dot_general | solution.py:42
  43.5 0.0 copy-start
  43.5 43.4 %all-gather.5.cloned.1.call-done = bf16[128,8192]{1,0:T(8,128)(2,1)} async-done(((bf16[128,2048]{1,0:T(8,128)(2,1)}), bf16[128,8192]{1,0:T(8,128)(2,1)}) %all-gather.5.cloned.1.call-update) | async-done | bytes 2097168 | tf_op jit(solution)/shard_map/all_gather | solution.py:35
  86.9 5.3 %fusion.2 = f32[128,512]{1,0:T(8,128)S(1)} fusion(bf16[128,8192]{1,0:T(8,128)(2,1)} %all-gather.5.cloned.1.call-done, bf16[8192,512]{1,0:T(8,128)(2,1)} %param.8), kind=kOutput, calls=%fused_computation.12 | convolution fusion | flops 1073741824 | bytes 10747904 | tf_op jit(solution)/shard_map/dot_general | solution.py:43
  92.2 0.8 pad_maximum_fusion
  93.0 0.0 reduce-scatter.3.cloned.1.call-update
  93.1 0.0 reduce-scatter.5.cloned.1.call-start
  93.1 0.0 copy-done
  93.1 0.1 dynamic_slice.3
  93.2 6.7 %reduce-scatter.3.cloned.1.call-done = f32[64,1024]{1,0:T(8,128)} async-done(((f32[128,1024]{1,0:T(8,128)}), f32[64,1024]{1,0:T(8,128)}) %reduce-scatter.3.cloned.1.call-update) | async-done | bytes 262160 | tf_op jit(solution)/shard_map/reduce_scatter | solution.py:39
  99.9 1.1 slice_reduce_fusion.1
  101.0 11.9 %all-reduce.1 = (f32[64]{0:T(128)S(1)}, f32[64]{0:T(128)S(1)}) all-reduce(f32[64]{0:T(128)S(1)} %get-tuple-element.6, f32[64]{0:T(128)S(1)} %get-tuple-element.5), channel_id=1, replica_groups=mesh['tok'=4,'hid'=2,'voc'=4] {'voc'}, use_global_device_ids=true, to_apply=%region_6.0 | all-reduce | flops 128 | bytes 1024 | tf_op jit(solution)/shard_map/pmax | solution.py:9
  112.9 1.2 multiply_reduce_fusion
  114.1 8.4 %all-reduce = (f32[64]{0:T(128)S(1)}, f32[64]{0:T(128)S(1)}, f32[64]{0:T(128)S(1)}) all-reduce(f32[64]{0:T(128)S(1)} %get-tuple-element.3, f32[64]{0:T(128)S(1)} %get-tuple-element.4, f32[64]{0:T(128)S(1)} %get-tuple-element.2), channel_id=1, replica_groups=mesh['tok'=4,'hid'=2,'voc'=4] {'voc'}, use_global_device_ids=true, to_apply=%region_8.0 | all-reduce | flops 192 | bytes 1536 | tf_op jit(solution)/shard_map/psum | solution.py:14
  122.5 0.6 add_reduce_fusion
  123.1 1.1 multiply_convert_fusion
  124.2 1.9 %all_gather.11 = bf16[128,512]{1,0:T(8,128)(2,1)S(1)} all-gather(bf16[64,512]{1,0:T(8,128)(2,1)S(1)} %multiply_convert_fusion), channel_id=1, replica_groups=mesh['tok'=4,'hid'=2,'voc'=4] {'hid'}, dimensions={0}, use_global_device_ids=true | all-gather | bytes 196608 | tf_op jit(solution)/shard_map/all_gather | solution.py:58
  126.1 5.0 %fusion.3 = f32[128,4096]{1,0:T(8,128)} fusion(bf16[128,512]{1,0:T(8,128)(2,1)S(1)} %all_gather.11, bf16[4096,512]{1,0:T(8,128)(2,1)} %param.7), kind=kOutput, calls=%fused_computation.13 | convolution fusion | flops 536870912 | bytes 6422528 | tf_op jit(solution)/shard_map/dot_general | solution.py:57
  131.1 0.0 reduce-scatter.5.cloned.1.call-update
  131.1 15.0 %psum.31 = f32[]{:T(128)} all-reduce(f32[]{:T(128)} %get-tuple-element.12), channel_id=1, replica_groups=mesh['tok'=4,'hid'=2,'voc'=4] {'tok','hid'}, use_global_device_ids=true, to_apply=%region_13.0 | all-reduce | flops 1 | bytes 8 | tf_op jit(solution)/shard_map/psum | solution.py:56
  146.8 27.8 %reduce-scatter.5.cloned.1.call-done = f32[128,1024]{1,0:T(8,128)} async-done(((f32[128,4096]{1,0:T(8,128)}), f32[128,1024]{1,0:T(8,128)}) %reduce-scatter.5.cloned.1.call-update) | async-done | bytes 524304 | tf_op jit(solution)/shard_map/reduce_scatter | solution.py:63
  174.5 1.8 convert_element_type.7
Async XLA Ops:
  7.2 33.1 %all-gather.3.cloned.1.call-start = ((), (), s32[]{:S(2)}) async-start(), calls=%async_computation.2 | async-start | bytes 1310720 | tf_op jit(solution)/shard_map/all_gather | solution.py:34
  7.9 79.0 %all-gather.5.cloned.1.call-start = ((), (), s32[]{:S(2)}) async-start(), calls=%async_computation.3 | async-start | bytes 2621440 | tf_op jit(solution)/shard_map/all_gather | solution.py:35
  8.6 91.3 %reduce-scatter.3.cloned.1.call-start = ((), (), s32[]{:S(2)}) async-start(), calls=%async_computation.4 | async-start | bytes 786432 | tf_op jit(solution)/shard_map/reduce_scatter | solution.py:39
  43.5 49.6 %copy-start = (f32[128]{0:T(128)S(1)}, f32[128]{0:T(128)}, u32[]{:S(2)}) copy-start(f32[128]{0:T(128)} %param.9) | copy-start | bytes 1540
  93.1 81.5 %reduce-scatter.5.cloned.1.call-start = ((), (), s32[]{:S(2)}) async-start(), calls=%async_computation.5 | async-start | bytes 2621440 | tf_op jit(solution)/shard_map/reduce_scatter | solution.py:63
Sparse Core Ops, SparseCore 0:
  9.5 30.6 all-gather.2
  41.8 45.0 all-gather.4
  93.2 6.7 reduce-scatter.2
  131.3 43.2 reduce-scatter.4
where the time goes:
time: 184 us
  waiting for transfers between devices  111 us (60%)
  blocking collectives  37.2 us (20%)
  between operations  15.6 us (8%)
  matrix products  13.5 us (7%)
  other arithmetic  6.6 us (4%)
    all_gather x1, waiting for transfers between devices, shards(): lax.all_gather(teacher_hidden, 'voc', axis=1, tiled=True)  43.4 us
    all_gather x1, waiting for transfers between devices, shards(): lax.all_gather(student_hidden, 'voc', axis=1, tiled=True)  31.6 us
    reduce_scatter x1, waiting for transfers between devices, shards(): lax.psum_scatter(grad_terms, 'voc', scatter_dimension=1, tiled=True)  27.8 us
    psum x1, blocking collectives, shards(): loss_total = lax.psum(jnp.sum(divergence), ('tok', 'hid'))  15 us
    pmax x1, blocking collectives, divergence_terms(): lax.pmax((jnp.max(student_logits, axis=1), jnp.max(teacher_logits, axis=1...  11.9 us
    psum x1, blocking collectives, divergence_terms(): lax.psum((jnp.sum(scaled_student, axis=1), jnp.sum(scaled_teacher, axis=1...  8.37 us
    reduce_scatter x1, waiting for transfers between devices, shards(): lax.psum_scatter(jnp.concatenate([jnp.dot(student_block, student_head, pr...  6.73 us
    dot_general x1, matrix products, shards(): jnp.dot(teacher_block, teacher_head, preferred_element_type=jnp.float32)  5.27 us
  transfers between devices with their start and end apart: 4, of which 4 were waited for; matrix products, arithmetic and copies ran while one was open for 2% of the time, Pallas kernels for 0%

commit v1 on v0

--- a/solution.py
+++ b/solution.py
@@ -2,6 +2,12 @@
 import jax.numpy as jnp
 from jax import lax
 from jax.sharding import PartitionSpec as P
+
+
+def gathered_along(x, name, d):
+    parts = lax.all_gather(x, name, axis=0, tiled=False)
+    out = jnp.concatenate(parts, axis=d)
+    return out
 
 
 def divergence_terms(student_logits, teacher_logits, weights):
@@ -32,7 +38,7 @@
 def shards(student_hidden, teacher_hidden, student_head, teacher_head, loss_weight):
     student_block, teacher_block = (
         lax.all_gather(student_hidden, "voc", axis=1, tiled=True),
-        lax.all_gather(teacher_hidden, "voc", axis=1, tiled=True),
+        gathered_along(teacher_hidden, "voc", 1),
     )
     vocab_local = student_head.shape[1]
     row_count = student_block.shape[0] // lax.axis_size("hid")

time: 184 us -> 187 us (1.016)
  local copies, waits for them, and re-layouts: 0.08 us -> 3.11 us
    reshape x0 -> x1, local copies, waits for them, and re-layouts: none -> 3.03 us  [gathered_along(): out = jnp.concatenate(parts, axis=d)]
where the time goes in v1:
time: 187 us; the launch traced here: 186 us
  waiting for transfers between devices  111 us (59%)
  blocking collectives  37.2 us (20%)
  between operations  15.6 us (8%)
  matrix products  12.9 us (7%)
  other arithmetic  6.6 us (4%)
  local copies, waits for them, and re-layouts  3.11 us (2%)
    all_gather x1, waiting for transfers between devices, gathered_along(): parts = lax.all_gather(x, name, axis=0, tiled=False)  43.4 us
    all_gather x1, waiting for transfers between devices, shards(): lax.all_gather(student_hidden, 'voc', axis=1, tiled=True)  31.6 us
    reduce_scatter x1, waiting for transfers between devices, shards(): lax.psum_scatter(grad_terms, 'voc', scatter_dimension=1, tiled=True)  27.8 us
    psum x1, blocking collectives, shards(): loss_total = lax.psum(jnp.sum(divergence), ('tok', 'hid'))  15 us
    pmax x1, blocking collectives, divergence_terms(): lax.pmax((jnp.max(student_logits, axis=1), jnp.max(teacher_logits, axis=1...  11.9 us
    psum x1, blocking collectives, divergence_terms(): lax.psum((jnp.sum(scaled_student, axis=1), jnp.sum(scaled_teacher, axis=1...  8.37 us
    reduce_scatter x1, waiting for transfers between devices, shards(): lax.psum_scatter(jnp.concatenate([jnp.dot(student_block, student_head, pr...  6.73 us
    dot_general x1, matrix products, shards(): lax.dot_general(lax.all_gather(scaled_gap, 'hid', axis=0, tiled=True), st...  5.01 us
  transfers between devices with their start and end apart: 4, of which 4 were waited for; matrix products, arithmetic and copies ran while one was open for 2% of the time, Pallas kernels for 0%

profile of v1, /device:TPU:0, one launch (start us, length us, event | category | flops | bytes accessed | tf_op | source)
XLA Modules:
  0.0 186.4 jit_solution(15193968785499936180)
XLA Ops:
  7.2 0.0 all-gather.4.cloned.1.call-start
  7.2 0.7 all-gather.4.cloned.1.call-update
  7.9 0.0 all-gather.6.cloned.1.call-start
  7.9 0.7 all-gather.6.cloned.1.call-update
  8.6 0.0 reduce-scatter.3.cloned.1.call-start
  8.7 31.6 %all-gather.4.cloned.1.call-done = bf16[128,4096]{1,0:T(8,128)(2,1)} async-done(((bf16[128,1024]{1,0:T(8,128)(2,1)}), bf16[128,4096]{1,0:T(8,128)(2,1)}) %all-gather.4.cloned.1.call-update) | async-done | bytes 1048592 | tf_op jit(solution)/shard_map/all_gather | solution.py:40
  40.3 3.2 %fusion.1 = f32[128,512]{1,0:T(8,128)S(1)} fusion(bf16[128,4096]{1,0:T(8,128)(2,1)} %all-gather.4.cloned.1.call-done, bf16[4096,512]{1,0:T(8,128)(2,1)} %param.7), kind=kOutput, calls=%fused_computation.11 | convolution fusion | flops 536870912 | bytes 5505024 | tf_op jit(solution)/shard_map/dot_general | solution.py:48
  43.5 43.4 %all-gather.6.cloned.1.call-done = bf16[512,2048]{1,0:T(8,128)(2,1)} async-done(((bf16[128,2048]{1,0:T(8,128)(2,1)}), bf16[512,2048]{1,0:T(8,128)(2,1)}) %all-gather.6.cloned.1.call-update) | async-done | bytes 2097168 | tf_op jit(solution)/shard_map/all_gather | solution.py:8
  86.9 3.0 %copy.7 = bf16[128,4,2048]{0,2,1:T(8,128)(2,1)S(1)} copy(bf16[128,4,2048]{2,0,1:T(8,128)(2,1)} %bitcast.11) | data formatting | bytes 4194304 | tf_op jit(solution)/shard_map/reshape | solution.py:9
  90.0 0.0 copy-start
  90.0 4.7 %fusion.2 = f32[128,512]{1,0:T(8,128)S(1)} fusion(bf16[128,8192]{0,1:T(8,128)(2,1)S(1)} %bitcast.10, bf16[8192,512]{1,0:T(8,128)(2,1)} %param.8), kind=kOutput, calls=%fused_computation.12 | convolution fusion | flops 1073741824 | bytes 10747904 | tf_op jit(solution)/shard_map/dot_general | solution.py:49
  94.6 0.8 pad_maximum_fusion
  95.5 0.0 reduce-scatter.3.cloned.1.call-update
  95.5 0.0 reduce-scatter.5.cloned.1.call-start
  95.6 0.0 copy-done
  95.6 0.1 dynamic_slice.3
  95.6 6.7 %reduce-scatter.3.cloned.1.call-done = f32[64,1024]{1,0:T(8,128)} async-done(((f32[128,1024]{1,0:T(8,128)}), f32[64,1024]{1,0:T(8,128)}) %reduce-scatter.3.cloned.1.call-update) | async-done | bytes 262160 | tf_op jit(solution)/shard_map/reduce_scatter | solution.py:45
  102.4 1.1 slice_reduce_fusion.1
  103.5 11.9 %all-reduce.1 = (f32[64]{0:T(128)S(1)}, f32[64]{0:T(128)S(1)}) all-reduce(f32[64]{0:T(128)S(1)} %get-tuple-element.6, f32[64]{0:T(128)S(1)} %get-tuple-element.5), channel_id=1, replica_groups=mesh['tok'=4,'hid'=2,'voc'=4] {'voc'}, use_global_device_ids=true, to_apply=%region_6.0 | all-reduce | flops 128 | bytes 1024 | tf_op jit(solution)/shard_map/pmax | solution.py:15
  115.4 1.2 multiply_reduce_fusion
  116.6 8.4 %all-reduce = (f32[64]{0:T(128)S(1)}, f32[64]{0:T(128)S(1)}, f32[64]{0:T(128)S(1)}) all-reduce(f32[64]{0:T(128)S(1)} %get-tuple-element.3, f32[64]{0:T(128)S(1)} %get-tuple-element.4, f32[64]{0:T(128)S(1)} %get-tuple-element.2), channel_id=1, replica_groups=mesh['tok'=4,'hid'=2,'voc'=4] {'voc'}, use_global_device_ids=true, to_apply=%region_8.0 | all-reduce | flops 192 | bytes 1536 | tf_op jit(solution)/shard_map/psum | solution.py:20
  125.0 0.6 add_reduce_fusion
  125.6 1.1 multiply_convert_fusion
  126.7 1.9 %all_gather.15 = bf16[128,512]{1,0:T(8,128)(2,1)S(1)} all-gather(bf16[64,512]{1,0:T(8,128)(2,1)S(1)} %multiply_convert_fusion), channel_id=1, replica_groups=mesh['tok'=4,'hid'=2,'voc'=4] {'hid'}, dimensions={0}, use_global_device_ids=true | all-gather | bytes 196608 | tf_op jit(solution)/shard_map/all_gather | solution.py:64
  128.6 5.0 %fusion.3 = f32[128,4096]{1,0:T(8,128)} fusion(bf16[128,512]{1,0:T(8,128)(2,1)S(1)} %all_gather.15, bf16[4096,512]{1,0:T(8,128)(2,1)} %param.7), kind=kOutput, calls=%fused_computation.13 | convolution fusion | flops 536870912 | bytes 6422528 | tf_op jit(solution)/shard_map/dot_general | solution.py:63
  133.6 0.0 reduce-scatter.5.cloned.1.call-update
  133.6 15.0 %psum.31 = f32[]{:T(128)} all-reduce(f32[]{:T(128)} %get-tuple-element.12), channel_id=1, replica_groups=mesh['tok'=4,'hid'=2,'voc'=4] {'tok','hid'}, use_global_device_ids=true, to_apply=%region_13.0 | all-reduce | flops 1 | bytes 8 | tf_op jit(solution)/shard_map/psum | solution.py:62
  149.2 27.8 %reduce-scatter.5.cloned.1.call-done = f32[128,1024]{1,0:T(8,128)} async-done(((f32[128,4096]{1,0:T(8,128)}), f32[128,1024]{1,0:T(8,128)}) %reduce-scatter.5.cloned.1.call-update) | async-done | bytes 524304 | tf_op jit(solution)/shard_map/reduce_scatter | solution.py:69
  177.0 1.8 convert_element_type.7
Async XLA Ops:
  7.2 33.1 %all-gather.4.cloned.1.call-start = ((), (), s32[]{:S(2)}) async-start(), calls=%async_computation.2 | async-start | bytes 1310720 | tf_op jit(solution)/shard_map/all_gather | solution.py:40
  7.9 79.0 %all-gather.6.cloned.1.call-start = ((), (), s32[]{:S(2)}) async-start(), calls=%async_computation.5 | async-start | bytes 2621440 | tf_op jit(solution)/shard_map/all_gather | solution.py:8
  8.6 93.7 %reduce-scatter.3.cloned.1.call-start = ((), (), s32[]{:S(2)}) async-start(), calls=%async_computation.3 | async-start | bytes 786432 | tf_op jit(solution)/shard_map/reduce_scatter | solution.py:45
  90.0 5.6 %copy-start = (f32[128]{0:T(128)S(1)}, f32[128]{0:T(128)}, u32[]{:S(2)}) copy-start(f32[128]{0:T(128)} %param.9) | copy-start | bytes 1540
  95.5 81.5 %reduce-scatter.5.cloned.1.call-start = ((), (), s32[]{:S(2)}) async-start(), calls=%async_computation.4 | async-start | bytes 2621440 | tf_op jit(solution)/shard_map/reduce_scatter | solution.py:69
Sparse Core Ops, SparseCore 0:
  9.5 30.6 all-gather.3
  41.8 45.0 all-gather.5
  95.6 6.7 reduce-scatter.2
  133.7 43.2 reduce-scatter.4
